TPU v7x, 16 devices: a 4x2x1 block of a 4x4x8 slice. The times are simulated.
16 devices in a mesh: dp: 2 (over y, z), tp: 8 (over x, core).
Axes of the slice: x: 4, y: 2, z: 1, core: 2. Of those that a mesh axis runs over, the one named last changes fastest.
The devices are a block of a 4x4x8 slice.
Arguments:
- x: bfloat16 [4096, 4096], P(('dp', 'tp')), parts along dimension 0
- w_gate: bfloat16 [4096, 14336], P(None, 'tp')
- w_up: bfloat16 [4096, 14336], P(None, 'tp')
- w_down: bfloat16 [14336, 4096], P('tp')
Outputs:
- output: bfloat16 [4096, 4096], P(('dp', 'tp')), parts along dimension 0
There are 2 independent parts. A program takes and returns all parts, laid end to end along the dimension named above; an argument that names none is the same for every part.
All inputs are finite; a program needn't handle non-finite values.
Results may differ from a plain program's by a relative error of at most 0.016.
Values are sent between devices in bfloat16 or wider.
A program may use at most 768 MiB of HBM per device.

v0:
```python
import jax
import jax.numpy as jnp
from jax import lax
from jax.sharding import PartitionSpec as P


def solution(mesh):
    def step(x, w_gate, w_up, w_down):
        rows = lax.all_gather(x, "tp", axis=0, tiled=True)
        gate = jnp.dot(rows, w_gate, preferred_element_type=jnp.float32)
        up = jnp.dot(rows, w_up, preferred_element_type=jnp.float32)
        hidden = (jax.nn.silu(gate) * up).astype(jnp.bfloat16)
        term = jnp.dot(hidden, w_down, preferred_element_type=jnp.float32).astype(jnp.bfloat16)
        return lax.psum_scatter(term, "tp", scatter_dimension=0, tiled=True)

    return jax.shard_map(
        step,
        mesh=mesh,
        in_specs=(P(("dp", "tp"), None), P(None, "tp"), P(None, "tp"), P("tp", None)),
        out_specs=P(("dp", "tp"), None),
        check_vma=False,
    )
```

profile of v0, /device:TPU:112, one launch (start us, length us, event | category | flops | bytes accessed | tf_op | source)
XLA Modules:
  0.0 301.9 jit_solution(11681601007545624411)
XLA Ops:
  6.5 0.0 all-gather.2.cloned.1.call-start
  6.6 0.7 all-gather.2.cloned.1.call-update
  7.3 0.1 reduce-scatter.2.cloned.1.call-start
  7.4 85.5 %all-gather.2.cloned.1.call-done = bf16[2048,4096]{1,0:T(8,128)(2,1)} async-done(((bf16[256,4096]{1,0:T(8,128)(2,1)}), bf16[2048,4096]{1,0:T(8,128)(2,1)}) %all-gather.2.cloned.1.call-update) | async-done | bytes 16777232 | tf_op jit(solution)/shard_map/all_gather | solution.py:9
  92.9 39.3 %fusion = f32[2048,1792]{1,0:T(8,128)} fusion(bf16[2048,4096]{1,0:T(8,128)(2,1)} %all-gather.2.cloned.1.call-done, bf16[4096,1792]{1,0:T(8,128)(2,1)} %param.5), kind=kOutput, calls=%fused_computation.2 | convolution fusion | flops 30064771072 | bytes 46137344 | tf_op jit(solution)/shard_map/dot_general | solution.py:10
  132.2 38.9 %multiply_convert_fusion = bf16[2048,1792]{1,0:T(8,128)(2,1)S(1)} fusion(f32[2048,1792]{1,0:T(8,128)} %fusion, bf16[2048,4096]{1,0:T(8,128)(2,1)} %all-gather.2.cloned.1.call-done, bf16[4096,1792]{1,0:T(8,128)(2,1)} %param.6), kind=kOutput, calls=%fused_computation.1 | convolution fusion | flops 30086791168 | bytes 53477376 | tf_op jit(solution)/shard_map/dot_general | solution.py:11
  171.1 35.4 %convolution_convert_fusion = bf16[2048,4096]{1,0:T(8,128)(2,1)} fusion(bf16[2048,1792]{1,0:T(8,128)(2,1)S(1)} %multiply_convert_fusion, bf16[1792,4096]{1,0:T(8,128)(2,1)} %param.7), kind=kOutput, calls=%fused_computation | convolution fusion | flops 30073159680 | bytes 38797312 | tf_op jit(solution)/shard_map/dot_general | solution.py:13
  206.5 0.1 reduce-scatter.2.cloned.1.call-update
  206.6 88.4 %reduce-scatter.2.cloned.1.call-done = bf16[256,4096]{1,0:T(8,128)(2,1)} async-done(((bf16[2048,4096]{1,0:T(8,128)(2,1)}), bf16[256,4096]{1,0:T(8,128)(2,1)}) %reduce-scatter.2.cloned.1.call-update) | async-done | bytes 2097168 | tf_op jit(solution)/shard_map/reduce_scatter | solution.py:14
Async XLA Ops:
  6.5 86.4 %all-gather.2.cloned.1.call-start = ((), (), s32[]{:S(2)}) async-start(), calls=%async_computation.1 | async-start | bytes 18874368 | tf_op jit(solution)/shard_map/all_gather | solution.py:9
  7.3 287.7 %reduce-scatter.2.cloned.1.call-start = ((), (), s32[]{:S(2)}) async-start(), calls=%async_computation.2 | async-start | bytes 18874368 | tf_op jit(solution)/shard_map/reduce_scatter | solution.py:14
Sparse Core Ops, SparseCore 0:
  8.9 83.9 all-gather.1
  206.7 88.2 reduce-scatter.1
where the time goes:
time: 302 us
  waiting for transfers between devices  175 us (58%)
  matrix products  114 us (38%)
  between operations  13.4 us (4%)
    reduce_scatter x1, waiting for transfers between devices, step(): return lax.psum_scatter(term, 'tp', scatter_dimension=0, tiled=True)  88.4 us
    all_gather x1, waiting for transfers between devices, step(): rows = lax.all_gather(x, 'tp', axis=0, tiled=True)  85.5 us
    dot_general x1, matrix products, step(): gate = jnp.dot(rows, w_gate, preferred_element_type=jnp.float32)  39.3 us
    dot_general x1, matrix products, step(): up = jnp.dot(rows, w_up, preferred_element_type=jnp.float32)  38.9 us
    dot_general x1, matrix products, step(): jnp.dot(hidden, w_down, preferred_element_type=jnp.float32)  35.4 us
  transfers between devices with their start and end apart: 2, of which 2 were waited for; matrix products, arithmetic and copies ran while one was open for 0% of the time, Pallas kernels for 0%

commit v1 on v0

v1 whole, which is shorter than its diff:
```python
import functools

import jax
import jax.numpy as jnp
from jax import lax
from jax.experimental import pallas as pl
from jax.experimental.pallas import tpu as pltpu
from jax.sharding import PartitionSpec as P

MESH = pl.DeviceIdType.MESH
BF16, F32 = jnp.bfloat16, jnp.float32
BLOCKS = 4
PIECES = 4
FT = 256
NT = 4

LAND = ((1, 0), (0, 1), (1, 0))


def kernel(n, x_ref, wg_ref, wu_ref, wd_ref, y_ref, xs, wg, wu, wd, h, mine, acc, give, got, arrived,
           in_sem, w_sem, wd_sem, ag_s, ag_r, dx_s, dx_r, d2_s, d2_r, rs_s, rs_r, y_sem):
    me = lax.axis_index("tp")
    chip, core = me // 2, me % 2
    chips = n // 2
    ring = (((chip + 1) % chips) * 2 + core, ((chip + chips - 1) % chips) * 2 + core)
    partner = chip * 2 + 1 - core

    rows, depth = x_ref.shape
    half = rows // 2
    piece = half // PIECES
    steps = wg_ref.shape[1] // FT
    cols = depth // NT

    def remote(src, dst, send, recv, to):
        return pltpu.make_async_remote_copy(
            src_ref=src, dst_ref=dst, send_sem=send, recv_sem=recv, device_id={"tp": to}, device_id_type=MESH
        )

    def load_x(q):
        at = pl.ds(q * piece, piece)
        return pltpu.make_async_copy(x_ref.at[at], xs.at[0, at], in_sem.at[q])

    def gather(s, d, p):
        to = LAND[s][d] * half + p * piece
        if s == 0:
            src = xs.at[0, pl.ds(d * half + p * piece, piece)]
        elif s == 1:
            src = xs.at[1, pl.ds(LAND[0][d] * half + p * piece, piece)]
        else:
            src = xs.at[0, pl.ds((1 - d) * half + p * piece, piece)]
        return remote(src, xs.at[s + 1, pl.ds(to, piece)], ag_s.at[s, d, p], ag_r.at[s, d, p], ring[d])

    def share(b, q):
        return remote(
            xs.at[b, pl.ds(q * piece, piece)], xs.at[b, pl.ds(rows + q * piece, piece)],
            dx_s.at[b, q], dx_r.at[b, q], partner,
        )

    def pass_on(s, p):
        for d in range(2):
            gather(s, d, p).wait_recv()
            if s == 0:
                gather(1, d, p).start()
            share(s + 1, LAND[s][d] * PIECES + p).start()
        if s == 0 and p == PIECES - 1:
            for q in range(PIECES):
                for d in range(2):
                    gather(2, d, q).start()

    def load_w(slot, i):
        at = pl.ds(pl.multiple_of(i * FT, FT), FT)
        return (
            pltpu.make_async_copy(wg_ref.at[:, at], wg.at[slot], w_sem.at[slot, 0]),
            pltpu.make_async_copy(wu_ref.at[:, at], wu.at[slot], w_sem.at[slot, 1]),
        )

    def tile(j):
        return pl.ds(pl.multiple_of(j * cols, cols), cols)

    def load_wd(slot, j):
        return pltpu.make_async_copy(wd_ref.at[:, tile(j)], wd.at[slot], wd_sem.at[slot])

    def hand(b, j):
        slot = j % 2
        return remote(give.at[slot], got.at[b, :, tile(j)], d2_s.at[slot], d2_r.at[b, j], partner)

    def reduce(r, d, j):
        src = xs.at[r + 1, pl.ds(rows + d * half, half), tile(j)]
        dst = arrived.at[r, pl.ds(d * half, half), tile(j)]
        return remote(src, dst, rs_s.at[r, d, j], rs_r.at[r, d, j], ring[d])

    def combine(b, j):
        hand(b, j).wait_recv()
        total = mine[j % 2] + got[b, :, tile(j)].astype(F32)
        if b == BLOCKS - 1:
            for d in range(2):
                reduce(1, d, j).wait_recv()
            total = total + arrived[1, :, tile(j)].astype(F32)
        xs[b, rows:, tile(j)] = total.astype(BF16)
        for d in range(2):
            reduce(b - 1, d, j).start()

    beside = {
        (0, 0, 2): [(0, 0)], (0, 0, 5): [(0, 1)], (0, 1, 0): [(0, 2)], (0, 1, 2): [(0, 3)],
        (1, 0, 1): [(1, 0)], (1, 0, 3): [(1, 1)], (1, 0, 5): [(1, 2)], (1, 1, 1): [(1, 3)],
        (2, 0, 0): [(2, 0)], (2, 0, 1): [(2, 1)], (2, 0, 3): [(2, 2)], (2, 0, 5): [(2, 3)],
    }

    def run_beside(b, phase, i):
        for (b_, phase_, step), pieces in beside.items():
            if (b_, phase_) == (b, phase):
                @pl.when(i == step)
                def _():
                    for s, p in pieces:
                        pass_on(s, p)

    for c in load_w(0, 0):
        c.start()
    for q in range(2 * PIECES):
        load_x(q).start()
    barrier = pltpu.get_barrier_semaphore()
    for to in (*ring, partner):
        pl.semaphore_signal(barrier, inc=1, device_id={"tp": to}, device_id_type=MESH)
    pl.semaphore_wait(barrier, 3)
    for p in range(PIECES):
        for d in range(2):
            q = d * PIECES + p
            load_x(q).wait()
            gather(0, d, p).start()
            share(0, q).start()

    for b in range(BLOCKS):
        for q in range(2 * PIECES):
            share(b, q).wait_recv()

        def project(i, _, b=b):
            at = b * steps + i
            slot = at % 2
            for c in load_w(slot, i):
                c.wait()

            @pl.when(at + 1 < BLOCKS * steps)
            def _():
                for c in load_w(1 - slot, (i + 1) % steps):
                    c.start()

            @pl.when(i == 0)
            def _():
                load_wd((b * NT) % 2, 0).start()

            if b >= 2:
                @pl.when(i == 1)
                def _():
                    combine(b - 1, NT - 1)

            run_beside(b, 0, i)
            x = xs[b]
            gate = jnp.dot(x, wg[slot], preferred_element_type=F32)
            up = jnp.dot(x, wu[slot], preferred_element_type=F32)
            h[:, pl.ds(pl.multiple_of(i * FT, FT), FT)] = (jax.nn.silu(gate) * up).astype(BF16)
            return 0

        lax.fori_loop(0, steps, project, 0)

        def contract(j, _, b=b):
            slot = (b * NT + j) % 2
            load_wd(slot, j).wait()

            @pl.when(j + 1 < NT)
            def _():
                load_wd(1 - slot, j + 1).start()

            run_beside(b, 1, j)
            if b > 0:
                @pl.when(j > 0)
                def _():
                    combine(b, j - 1)

            @pl.when(b * NT + j >= 2)
            def _():
                hand(b, j).wait_send()

            term = jnp.dot(h[...], wd[slot], preferred_element_type=F32)
            give[j % 2] = term[rows:].astype(BF16)
            if b == 0:
                acc[:, tile(j)] = term[:rows]
            else:
                mine[j % 2] = term[:rows]
            hand(b, j).start()
            return 0

        lax.fori_loop(0, NT, contract, 0)

    combine(BLOCKS - 1, NT - 1)

    def early(j, _):
        hand(0, j).wait_recv()
        for d in range(2):
            reduce(0, d, j).wait_recv()
        for d in range(2):
            at = pl.ds(d * half, half)
            other = pl.ds((1 - d) * half, half)
            acc[at, tile(j)] = (
                acc[at, tile(j)] + got[0, at, tile(j)].astype(F32) + arrived[0, other, tile(j)].astype(F32)
            )
        return 0

    lax.fori_loop(0, NT, early, 0)

    def store_y(j):
        return pltpu.make_async_copy(xs.at[0, rows:, tile(j)], y_ref.at[:, tile(j)], y_sem.at[j])

    def finish(j, _):
        for d in range(2):
            reduce(2, d, j).wait_recv()
        xs[0, rows:, tile(j)] = (acc[:, tile(j)] + arrived[2, :, tile(j)].astype(F32)).astype(BF16)
        store_y(j).start()
        return 0

    lax.fori_loop(0, NT, finish, 0)

    for j in range(NT):
        for d in range(2):
            for r in range(3):
                reduce(r, d, j).wait_send()
    for j in range(2):
        hand(BLOCKS - 1, j).wait_send()
    for s in range(3):
        for d in range(2):
            for p in range(PIECES):
                gather(s, d, p).wait_send()
    for b in range(BLOCKS):
        for q in range(2 * PIECES):
            share(b, q).wait_send()
    for j in range(NT):
        store_y(j).wait()


def solution(mesh):
    n = mesh.shape["tp"]

    def step(x, w_gate, w_up, w_down):
        rows, depth = x.shape
        units = w_gate.shape[1]
        cols = depth // NT
        dma = pltpu.SemaphoreType.DMA
        return pl.pallas_call(
            functools.partial(kernel, n),
            name="mlp",
            out_shape=jax.ShapeDtypeStruct((rows, depth), BF16),
            in_specs=[pl.BlockSpec(memory_space=pl.ANY)] * 4,
            out_specs=pl.BlockSpec(memory_space=pl.ANY),
            scratch_shapes=[
                pltpu.VMEM((BLOCKS, 2 * rows, depth), BF16),
                pltpu.VMEM((2, depth, FT), BF16),
                pltpu.VMEM((2, depth, FT), BF16),
                pltpu.VMEM((2, units, cols), BF16),
                pltpu.VMEM((2 * rows, units), BF16),
                pltpu.VMEM((2, rows, cols), F32),
                pltpu.VMEM((rows, depth), F32),
                pltpu.VMEM((2, rows, cols), BF16),
                pltpu.VMEM((BLOCKS, rows, depth), BF16),
                pltpu.VMEM((3, rows, depth), BF16),
                dma((2 * PIECES,)), dma((2, 2)), dma((2,)),
                dma((3, 2, PIECES)), dma((3, 2, PIECES)),
                dma((BLOCKS, 2 * PIECES)), dma((BLOCKS, 2 * PIECES)),
                dma((2,)), dma((BLOCKS, NT)),
                dma((3, 2, NT)), dma((3, 2, NT)), dma((NT,)),
            ],
            compiler_params=pltpu.CompilerParams(
                collective_id=0, has_side_effects=True, vmem_limit_bytes=67043328
            ),
        )(x, w_gate, w_up, w_down)

    return jax.shard_map(
        step,
        mesh=mesh,
        in_specs=(P(("dp", "tp"), None), P(None, "tp"), P(None, "tp"), P("tp", None)),
        out_specs=P(("dp", "tp"), None),
        check_vma=False,
    )
```

time: 302 us -> 149 us (0.49)
  waiting for transfers between devices: 175 us -> 0 us
  Pallas kernels: 0 us -> 146 us
  matrix products: 114 us -> 0 us
  between operations: 13.4 us -> 0.01 us
  local copies, waits for them, and re-layouts: 0 us -> 3.13 us
    pallas_call x0 -> x1, Pallas kernels: none -> 146 us  [step(): pl.pallas_call(functools.partial(kernel, n), name='mlp', out_shape=jax.Sh...]
    dot_general x3 -> x0, matrix products: 114 us -> none  [the longest x1 39.3 us: step(): gate = jnp.dot(rows, w_gate, preferred_element_type=jnp.float32)]
    reduce_scatter x1 -> x0, waiting for transfers between devices: 88.4 us -> none  [step(): return lax.psum_scatter(term, 'tp', scatter_dimension=0, tiled=True)]
    all_gather x1 -> x0, waiting for transfers between devices: 85.5 us -> none  [step(): rows = lax.all_gather(x, 'tp', axis=0, tiled=True)]
    unnamed x0 -> x1, local copies, waits for them, and re-layouts: none -> 3.13 us
  transfers between devices with their start and end apart: 2 -> 0, of which waited for: 2 -> 0; matrix products, arithmetic and copies ran while one was open for 0% -> 0% of each run, Pallas kernels for 0% -> 0%
where the time goes in v1:
time: 149 us
  Pallas kernels  146 us (98%)
  local copies, waits for them, and re-layouts  3.13 us (2%)
    pallas_call x1, Pallas kernels, step(): pl.pallas_call(functools.partial(kernel, n), name='mlp', out_shape=jax.Sh...  146 us
    unnamed x1, local copies, waits for them, and re-layouts  3.13 us

profile of v1, /device:TPU:112, one launch (start us, length us, event | category | flops | bytes accessed | tf_op | source)
XLA Modules:
  0.0 149.3 jit_solution(15368315624745746645)
XLA Ops:
  0.0 146.2 %mlp.1 = bf16[256,4096]{1,0:T(8,128)(2,1)} custom-call(bf16[256,4096]{1,0:T(8,128)(2,1)} %x_ref.1, bf16[4096,1792]{1,0:T(8,128)(2,1)} %wg_ref.1, bf16[4096,1792]{1,0:T(8,128)(2,1)} %wu_ref.1, bf16[1792,4096]{1,0:T(8,128)(2,1)} %wd_ref.1), custom_call_target="tpu_custom_call" | custom-call | tf_op jit(solution)/shard_map/mlp/pallas_call | solution.py:247
  146.2 3.1 %copy.6 = bf16[256,4096]{1,0:T(8,128)(2,1)} copy(bf16[256,4096]{1,0:T(8,128)(2,1)} %mlp.1) | data formatting | bytes 4194304

commit v2 on v1

--- a/solution.py
+++ b/solution.py
@@ -18,7 +18,7 @@
 
 
 def kernel(n, x_ref, wg_ref, wu_ref, wd_ref, y_ref, xs, wg, wu, wd, h, mine, acc, give, got, arrived,
-           in_sem, w_sem, wd_sem, ag_s, ag_r, dx_s, dx_r, d2_s, d2_r, rs_s, rs_r, y_sem):
+           in_sem, w_sem, wd_sem, ag_s, ag_r, dx_s, dx_r, d2_s, d2_r, rs_s, n1_r, rs_r, y_sem):
     me = lax.axis_index("tp")
     chip, core = me // 2, me % 2
     chips = n // 2
@@ -48,13 +48,16 @@
             src = xs.at[1, pl.ds(LAND[0][d] * half + p * piece, piece)]
         else:
             src = xs.at[0, pl.ds((1 - d) * half + p * piece, piece)]
-        return remote(src, xs.at[s + 1, pl.ds(to, piece)], ag_s.at[s, d, p], ag_r.at[s, d, p], ring[d])
+        return remote(src, xs.at[s + 1, pl.ds(to, piece)], ag_s, ag_r.at[s, d, p], ring[d])
 
     def share(b, q):
         return remote(
             xs.at[b, pl.ds(q * piece, piece)], xs.at[b, pl.ds(rows + q * piece, piece)],
-            dx_s.at[b, q], dx_r.at[b, q], partner,
+            dx_s, dx_r.at[b], partner,
         )
+
+    def landed(ref, sem):
+        pltpu.make_async_copy(ref, ref, sem).wait()
 
     def pass_on(s, p):
         for d in range(2):
@@ -87,7 +90,7 @@
     def reduce(r, d, j):
         src = xs.at[r + 1, pl.ds(rows + d * half, half), tile(j)]
         dst = arrived.at[r, pl.ds(d * half, half), tile(j)]
-        return remote(src, dst, rs_s.at[r, d, j], rs_r.at[r, d, j], ring[d])
+        return remote(src, dst, rs_s, n1_r if r == 0 else rs_r.at[r - 1, d, j], ring[d])
 
     def combine(b, j):
         hand(b, j).wait_recv()
@@ -130,8 +133,7 @@
             share(0, q).start()
 
     for b in range(BLOCKS):
-        for q in range(2 * PIECES):
-            share(b, q).wait_recv()
+        landed(xs.at[b, pl.ds(rows, rows)], dx_r.at[b])
 
         def project(i, _, b=b):
             at = b * steps + i
@@ -171,10 +173,6 @@
                 load_wd(1 - slot, j + 1).start()
 
             run_beside(b, 1, j)
-            if b > 0:
-                @pl.when(j > 0)
-                def _():
-                    combine(b, j - 1)
 
             @pl.when(b * NT + j >= 2)
             def _():
@@ -187,16 +185,21 @@
             else:
                 mine[j % 2] = term[:rows]
             hand(b, j).start()
+            if b > 0:
+                @pl.when(j > 0)
+                def _():
+                    combine(b, j - 1)
+
             return 0
 
         lax.fori_loop(0, NT, contract, 0)
 
     combine(BLOCKS - 1, NT - 1)
+
+    landed(arrived.at[0], n1_r)
 
     def early(j, _):
         hand(0, j).wait_recv()
-        for d in range(2):
-            reduce(0, d, j).wait_recv()
         for d in range(2):
             at = pl.ds(d * half, half)
             other = pl.ds((1 - d) * half, half)
@@ -208,7 +211,7 @@
     lax.fori_loop(0, NT, early, 0)
 
     def store_y(j):
-        return pltpu.make_async_copy(xs.at[0, rows:, tile(j)], y_ref.at[:, tile(j)], y_sem.at[j])
+        return pltpu.make_async_copy(xs.at[0, rows:, tile(j)], y_ref.at[:, tile(j)], y_sem)
 
     def finish(j, _):
         for d in range(2):
@@ -219,21 +222,12 @@
 
     lax.fori_loop(0, NT, finish, 0)
 
-    for j in range(NT):
-        for d in range(2):
-            for r in range(3):
-                reduce(r, d, j).wait_send()
+    landed(arrived, rs_s)
+    landed(arrived, ag_s)
     for j in range(2):
         hand(BLOCKS - 1, j).wait_send()
-    for s in range(3):
-        for d in range(2):
-            for p in range(PIECES):
-                gather(s, d, p).wait_send()
-    for b in range(BLOCKS):
-        for q in range(2 * PIECES):
-            share(b, q).wait_send()
-    for j in range(NT):
-        store_y(j).wait()
+    landed(xs.at[:, pl.ds(0, rows)], dx_s)
+    landed(xs.at[0, pl.ds(rows, rows)], y_sem)
 
 
 def solution(mesh):
@@ -262,10 +256,10 @@
                 pltpu.VMEM((BLOCKS, rows, depth), BF16),
                 pltpu.VMEM((3, rows, depth), BF16),
                 dma((2 * PIECES,)), dma((2, 2)), dma((2,)),
-                dma((3, 2, PIECES)), dma((3, 2, PIECES)),
-                dma((BLOCKS, 2 * PIECES)), dma((BLOCKS, 2 * PIECES)),
+                dma, dma((3, 2, PIECES)),
+                dma, dma((BLOCKS,)),
                 dma((2,)), dma((BLOCKS, NT)),
-                dma((3, 2, NT)), dma((3, 2, NT)), dma((NT,)),
+                dma, dma, dma((2, 2, NT)), dma,
             ],
             compiler_params=pltpu.CompilerParams(
                 collective_id=0, has_side_effects=True, vmem_limit_bytes=67043328

time: 149 us -> 145 us (0.973)
  Pallas kernels: 146 us -> 142 us
    pallas_call x1, Pallas kernels: 146 us -> 142 us  [step(): pl.pallas_call(functools.partial(kernel, n), name='mlp', out_shape=jax.Sh...]
where the time goes in v2:
time: 145 us
  Pallas kernels  142 us (98%)
  local copies, waits for them, and re-layouts  3.13 us (2%)
    pallas_call x1, Pallas kernels, step(): pl.pallas_call(functools.partial(kernel, n), name='mlp', out_shape=jax.Sh...  142 us
    unnamed x1, local copies, waits for them, and re-layouts  3.13 us

profile of v2, /device:TPU:112, one launch (start us, length us, event | category | flops | bytes accessed | tf_op | source)
XLA Modules:
  0.0 145.2 jit_solution(8797953262774424084)
XLA Ops:
  0.0 142.1 %mlp.1 = bf16[256,4096]{1,0:T(8,128)(2,1)} custom-call(bf16[256,4096]{1,0:T(8,128)(2,1)} %x_ref.1, bf16[4096,1792]{1,0:T(8,128)(2,1)} %wg_ref.1, bf16[4096,1792]{1,0:T(8,128)(2,1)} %wu_ref.1, bf16[1792,4096]{1,0:T(8,128)(2,1)} %wd_ref.1), custom_call_target="tpu_custom_call" | custom-call | tf_op jit(solution)/shard_map/mlp/pallas_call | solution.py:241
  142.1 3.1 %copy.6 = bf16[256,4096]{1,0:T(8,128)(2,1)} copy(bf16[256,4096]{1,0:T(8,128)(2,1)} %mlp.1) | data formatting | bytes 4194304

commit v3 on v2

--- a/solution.py
+++ b/solution.py
@@ -18,7 +18,7 @@
 
 
 def kernel(n, x_ref, wg_ref, wu_ref, wd_ref, y_ref, xs, wg, wu, wd, h, mine, acc, give, got, arrived,
-           in_sem, w_sem, wd_sem, ag_s, ag_r, dx_s, dx_r, d2_s, d2_r, rs_s, n1_r, rs_r, y_sem):
+           in_sem, w_sem, wd_sem, ag_s, ag_r, dx_s, dx_r, d2_s, d2_r, rs_s, n1_r, rs_r):
     me = lax.axis_index("tp")
     chip, core = me // 2, me % 2
     chips = n // 2
@@ -210,14 +210,10 @@
 
     lax.fori_loop(0, NT, early, 0)
 
-    def store_y(j):
-        return pltpu.make_async_copy(xs.at[0, rows:, tile(j)], y_ref.at[:, tile(j)], y_sem)
-
     def finish(j, _):
         for d in range(2):
             reduce(2, d, j).wait_recv()
-        xs[0, rows:, tile(j)] = (acc[:, tile(j)] + arrived[2, :, tile(j)].astype(F32)).astype(BF16)
-        store_y(j).start()
+        y_ref[:, tile(j)] = (acc[:, tile(j)] + arrived[2, :, tile(j)].astype(F32)).astype(BF16)
         return 0
 
     lax.fori_loop(0, NT, finish, 0)
@@ -227,7 +223,6 @@
     for j in range(2):
         hand(BLOCKS - 1, j).wait_send()
     landed(xs.at[:, pl.ds(0, rows)], dx_s)
-    landed(xs.at[0, pl.ds(rows, rows)], y_sem)
 
 
 def solution(mesh):
@@ -241,9 +236,9 @@
         return pl.pallas_call(
             functools.partial(kernel, n),
             name="mlp",
-            out_shape=jax.ShapeDtypeStruct((rows, depth), BF16),
+            out_shape=pltpu.VMEM((rows, depth), BF16),
             in_specs=[pl.BlockSpec(memory_space=pl.ANY)] * 4,
-            out_specs=pl.BlockSpec(memory_space=pl.ANY),
+            out_specs=pl.BlockSpec(memory_space=pltpu.VMEM),
             scratch_shapes=[
                 pltpu.VMEM((BLOCKS, 2 * rows, depth), BF16),
                 pltpu.VMEM((2, depth, FT), BF16),
@@ -259,10 +254,10 @@
                 dma, dma((3, 2, PIECES)),
                 dma, dma((BLOCKS,)),
                 dma((2,)), dma((BLOCKS, NT)),
-                dma, dma, dma((2, 2, NT)), dma,
+                dma, dma, dma((2, 2, NT)),
             ],
             compiler_params=pltpu.CompilerParams(
-                collective_id=0, has_side_effects=True, vmem_limit_bytes=67043328
+                collective_id=0, has_side_effects=True, vmem_limit_bytes=62914560
             ),
         )(x, w_gate, w_up, w_down)
 

time: 145 us -> 143 us (0.986)
  local copies, waits for them, and re-layouts: 3.13 us -> 1.32 us
    unnamed x1, local copies, waits for them, and re-layouts: 3.13 us -> 1.32 us
where the time goes in v3:
time: 143 us
  Pallas kernels  141 us (99%)
    pallas_call x1, Pallas kernels, step(): pl.pallas_call(functools.partial(kernel, n), name='mlp', out_shape=pltpu....  141 us

profile of v3, /device:TPU:112, one launch (start us, length us, event | category | flops | bytes accessed | tf_op | source)
XLA Modules:
  0.0 142.6 jit_solution(5558246406108778449)
XLA Ops:
  0.0 141.2 %mlp.1 = bf16[256,4096]{1,0:T(8,128)(2,1)S(1)} custom-call(bf16[256,4096]{1,0:T(8,128)(2,1)} %x_ref.1, bf16[4096,1792]{1,0:T(8,128)(2,1)} %wg_ref.1, bf16[4096,1792]{1,0:T(8,128)(2,1)} %wu_ref.1, bf16[1792,4096]{1,0:T(8,128)(2,1)} %wd_ref.1), custom_call_target="tpu_custom_call" | custom-call | tf_op jit(solution)/shard_map/mlp/pallas_call | solution.py:236
  141.2 1.3 copy.6

commit v4 on v3

--- a/solution.py
+++ b/solution.py
@@ -18,7 +18,7 @@
 
 
 def kernel(n, x_ref, wg_ref, wu_ref, wd_ref, y_ref, xs, wg, wu, wd, h, mine, acc, give, got, arrived,
-           in_sem, w_sem, wd_sem, ag_s, ag_r, dx_s, dx_r, d2_s, d2_r, rs_s, n1_r, rs_r):
+           in_sem, w_sem, wd_sem, ag_s, ag_r, dx_s, dx_r, d2_s, d0_r, d2_r, rs_s, n1_r, rs_r):
     me = lax.axis_index("tp")
     chip, core = me // 2, me % 2
     chips = n // 2
@@ -48,7 +48,7 @@
             src = xs.at[1, pl.ds(LAND[0][d] * half + p * piece, piece)]
         else:
             src = xs.at[0, pl.ds((1 - d) * half + p * piece, piece)]
-        return remote(src, xs.at[s + 1, pl.ds(to, piece)], ag_s, ag_r.at[s, d, p], ring[d])
+        return remote(src, xs.at[s + 1, pl.ds(to, piece)], ag_s, ag_r.at[p if s == 0 else PIECES + s - 1], ring[d])
 
     def share(b, q):
         return remote(
@@ -60,15 +60,19 @@
         pltpu.make_async_copy(ref, ref, sem).wait()
 
     def pass_on(s, p):
-        for d in range(2):
-            gather(s, d, p).wait_recv()
-            if s == 0:
+        if s == 0:
+            landed(xs.at[1, pl.ds(0, 2 * piece)], ag_r.at[p])
+            for d in range(2):
                 gather(1, d, p).start()
-            share(s + 1, LAND[s][d] * PIECES + p).start()
-        if s == 0 and p == PIECES - 1:
-            for q in range(PIECES):
-                for d in range(2):
-                    gather(2, d, q).start()
+                share(1, LAND[0][d] * PIECES + p).start()
+            if p == PIECES - 1:
+                for q in range(PIECES):
+                    for d in range(2):
+                        gather(2, d, q).start()
+        else:
+            landed(xs.at[s + 1, pl.ds(0, rows)], ag_r.at[PIECES + s - 1])
+            for q in range(2 * PIECES):
+                share(s + 1, q).start()
 
     def load_w(slot, i):
         at = pl.ds(pl.multiple_of(i * FT, FT), FT)
@@ -85,19 +89,18 @@
 
     def hand(b, j):
         slot = j % 2
-        return remote(give.at[slot], got.at[b, :, tile(j)], d2_s.at[slot], d2_r.at[b, j], partner)
+        return remote(give.at[slot], got.at[b, :, tile(j)], d2_s.at[slot], d0_r if b == 0 else d2_r.at[b - 1, j], partner)
 
     def reduce(r, d, j):
         src = xs.at[r + 1, pl.ds(rows + d * half, half), tile(j)]
         dst = arrived.at[r, pl.ds(d * half, half), tile(j)]
-        return remote(src, dst, rs_s, n1_r if r == 0 else rs_r.at[r - 1, d, j], ring[d])
+        return remote(src, dst, rs_s, n1_r if r == 0 else rs_r.at[r - 1, j], ring[d])
 
     def combine(b, j):
         hand(b, j).wait_recv()
         total = mine[j % 2] + got[b, :, tile(j)].astype(F32)
         if b == BLOCKS - 1:
-            for d in range(2):
-                reduce(1, d, j).wait_recv()
+            landed(arrived.at[1, :, tile(j)], rs_r.at[0, j])
             total = total + arrived[1, :, tile(j)].astype(F32)
         xs[b, rows:, tile(j)] = total.astype(BF16)
         for d in range(2):
@@ -105,8 +108,7 @@
 
     beside = {
         (0, 0, 2): [(0, 0)], (0, 0, 5): [(0, 1)], (0, 1, 0): [(0, 2)], (0, 1, 2): [(0, 3)],
-        (1, 0, 1): [(1, 0)], (1, 0, 3): [(1, 1)], (1, 0, 5): [(1, 2)], (1, 1, 1): [(1, 3)],
-        (2, 0, 0): [(2, 0)], (2, 0, 1): [(2, 1)], (2, 0, 3): [(2, 2)], (2, 0, 5): [(2, 3)],
+        (1, 1, 1): [(1, 0)], (2, 0, 6): [(2, 0)],
     }
 
     def run_beside(b, phase, i):
@@ -117,13 +119,12 @@
                     for s, p in pieces:
                         pass_on(s, p)
 
-    for c in load_w(0, 0):
-        c.start()
-    for q in range(2 * PIECES):
-        load_x(q).start()
     barrier = pltpu.get_barrier_semaphore()
     for to in (*ring, partner):
         pl.semaphore_signal(barrier, inc=1, device_id={"tp": to}, device_id_type=MESH)
+    for p in range(PIECES):
+        for d in range(2):
+            load_x(d * PIECES + p).start()
     pl.semaphore_wait(barrier, 3)
     for p in range(PIECES):
         for d in range(2):
@@ -131,6 +132,8 @@
             load_x(q).wait()
             gather(0, d, p).start()
             share(0, q).start()
+    for c in load_w(0, 0):
+        c.start()
 
     for b in range(BLOCKS):
         landed(xs.at[b, pl.ds(rows, rows)], dx_r.at[b])
@@ -196,10 +199,10 @@
 
     combine(BLOCKS - 1, NT - 1)
 
+    landed(got.at[0], d0_r)
     landed(arrived.at[0], n1_r)
 
     def early(j, _):
-        hand(0, j).wait_recv()
         for d in range(2):
             at = pl.ds(d * half, half)
             other = pl.ds((1 - d) * half, half)
@@ -211,8 +214,7 @@
     lax.fori_loop(0, NT, early, 0)
 
     def finish(j, _):
-        for d in range(2):
-            reduce(2, d, j).wait_recv()
+        landed(arrived.at[2, :, tile(j)], rs_r.at[1, j])
         y_ref[:, tile(j)] = (acc[:, tile(j)] + arrived[2, :, tile(j)].astype(F32)).astype(BF16)
         return 0
 
@@ -251,10 +253,10 @@
                 pltpu.VMEM((BLOCKS, rows, depth), BF16),
                 pltpu.VMEM((3, rows, depth), BF16),
                 dma((2 * PIECES,)), dma((2, 2)), dma((2,)),
-                dma, dma((3, 2, PIECES)),
+                dma, dma((PIECES + 2,)),
                 dma, dma((BLOCKS,)),
-                dma((2,)), dma((BLOCKS, NT)),
-                dma, dma, dma((2, 2, NT)),
+                dma((2,)), dma, dma((BLOCKS - 1, NT)),
+                dma, dma, dma((2, NT)),
             ],
             compiler_params=pltpu.CompilerParams(
                 collective_id=0, has_side_effects=True, vmem_limit_bytes=62914560

time: 143 us -> 142 us (level)
  no operation moved by 1% of the time
where the time goes in v4:
time: 142 us
  Pallas kernels  141 us (99%)
    pallas_call x1, Pallas kernels, step(): pl.pallas_call(functools.partial(kernel, n), name='mlp', out_shape=pltpu....  141 us

profile of v4, /device:TPU:112, one launch (start us, length us, event | category | flops | bytes accessed | tf_op | source)
XLA Modules:
  0.0 142.3 jit_solution(13174676683143366571)
XLA Ops:
  0.0 141.0 %mlp.1 = bf16[256,4096]{1,0:T(8,128)(2,1)S(1)} custom-call(bf16[256,4096]{1,0:T(8,128)(2,1)} %x_ref.1, bf16[4096,1792]{1,0:T(8,128)(2,1)} %wg_ref.1, bf16[4096,1792]{1,0:T(8,128)(2,1)} %wu_ref.1, bf16[1792,4096]{1,0:T(8,128)(2,1)} %wd_ref.1), custom_call_target="tpu_custom_call" | custom-call | tf_op jit(solution)/shard_map/mlp/pallas_call | solution.py:238
  141.0 1.3 copy.6

commit v5 on v4

--- a/solution.py
+++ b/solution.py
@@ -13,12 +13,13 @@
 PIECES = 4
 FT = 256
 NT = 4
+LAST = 256
 
 LAND = ((1, 0), (0, 1), (1, 0))
 
 
-def kernel(n, x_ref, wg_ref, wu_ref, wd_ref, y_ref, xs, wg, wu, wd, h, mine, acc, give, got, arrived,
-           in_sem, w_sem, wd_sem, ag_s, ag_r, dx_s, dx_r, d2_s, d0_r, d2_r, rs_s, n1_r, rs_r):
+def kernel(n, x_ref, wg_ref, wu_ref, wd_ref, y_ref, xs, wgu, wd, h, mine, acc, give, got, arrived,
+           in_sem, w_sem, wd_sem, ag_s, ag_r, dx_s, dx_r, d2_s, own_r, d2_r, rs_s, rs_r):
     me = lax.axis_index("tp")
     chip, core = me // 2, me % 2
     chips = n // 2
@@ -30,6 +31,7 @@
     piece = half // PIECES
     steps = wg_ref.shape[1] // FT
     cols = depth // NT
+    first, last = pl.ds(depth - cols, cols - LAST), pl.ds(depth - LAST, LAST)
 
     def remote(src, dst, send, recv, to):
         return pltpu.make_async_remote_copy(
@@ -38,7 +40,7 @@
 
     def load_x(q):
         at = pl.ds(q * piece, piece)
-        return pltpu.make_async_copy(x_ref.at[at], xs.at[0, at], in_sem.at[q])
+        return pltpu.make_async_copy(x_ref.at[at], xs.at[0, at], in_sem.at[0 if q % PIECES == 0 else 1])
 
     def gather(s, d, p):
         to = LAND[s][d] * half + p * piece
@@ -53,7 +55,7 @@
     def share(b, q):
         return remote(
             xs.at[b, pl.ds(q * piece, piece)], xs.at[b, pl.ds(rows + q * piece, piece)],
-            dx_s, dx_r.at[b], partner,
+            dx_s, dx_r.at[b % 2], partner,
         )
 
     def landed(ref, sem):
@@ -77,8 +79,8 @@
     def load_w(slot, i):
         at = pl.ds(pl.multiple_of(i * FT, FT), FT)
         return (
-            pltpu.make_async_copy(wg_ref.at[:, at], wg.at[slot], w_sem.at[slot, 0]),
-            pltpu.make_async_copy(wu_ref.at[:, at], wu.at[slot], w_sem.at[slot, 1]),
+            pltpu.make_async_copy(wg_ref.at[:, at], wgu.at[slot, 0], w_sem.at[slot]),
+            pltpu.make_async_copy(wu_ref.at[:, at], wgu.at[slot, 1], w_sem.at[slot]),
         )
 
     def tile(j):
@@ -89,22 +91,41 @@
 
     def hand(b, j):
         slot = j % 2
-        return remote(give.at[slot], got.at[b, :, tile(j)], d2_s.at[slot], d0_r if b == 0 else d2_r.at[b - 1, j], partner)
-
-    def reduce(r, d, j):
-        src = xs.at[r + 1, pl.ds(rows + d * half, half), tile(j)]
-        dst = arrived.at[r, pl.ds(d * half, half), tile(j)]
-        return remote(src, dst, rs_s, n1_r if r == 0 else rs_r.at[r - 1, j], ring[d])
+        return remote(give.at[slot], got.at[b, :, tile(j)], d2_s.at[slot], own_r if b == 0 else d2_r.at[b % 2, j], partner)
+
+    def reduce(r, d, columns, sem):
+        src = xs.at[r + 1, pl.ds(rows + d * half, half), columns]
+        dst = arrived.at[r, pl.ds(d * half, half), columns]
+        return remote(src, dst, rs_s, sem, ring[d])
+
+    def send_on(r, j):
+        if r < 2:
+            for d in range(2):
+                reduce(r, d, tile(j), own_r if r == 0 else rs_r.at[0, j // 2]).start()
+            return
+
+        @pl.when(j < NT - 1)
+        def _():
+            for d in range(2):
+                reduce(2, d, tile(j), rs_r.at[1, 0]).start()
+
+        @pl.when(j == NT - 1)
+        def _():
+            for columns, at in ((first, 0), (last, 1)):
+                for d in range(2):
+                    reduce(2, d, columns, rs_r.at[1, at]).start()
 
     def combine(b, j):
         hand(b, j).wait_recv()
         total = mine[j % 2] + got[b, :, tile(j)].astype(F32)
         if b == BLOCKS - 1:
-            landed(arrived.at[1, :, tile(j)], rs_r.at[0, j])
+            @pl.when(j % 2 == 0)
+            def _():
+                landed(arrived.at[1, :, pl.ds(0, 2 * cols)], rs_r.at[0, j // 2])
+
             total = total + arrived[1, :, tile(j)].astype(F32)
         xs[b, rows:, tile(j)] = total.astype(BF16)
-        for d in range(2):
-            reduce(b - 1, d, j).start()
+        send_on(b - 1, j)
 
     beside = {
         (0, 0, 2): [(0, 0)], (0, 0, 5): [(0, 1)], (0, 1, 0): [(0, 2)], (0, 1, 2): [(0, 3)],
@@ -127,22 +148,21 @@
             load_x(d * PIECES + p).start()
     pl.semaphore_wait(barrier, 3)
     for p in range(PIECES):
+        if p < 2:
+            landed(xs.at[0, pl.ds(0, 2 * (piece if p == 0 else half - piece))], in_sem.at[p])
         for d in range(2):
-            q = d * PIECES + p
-            load_x(q).wait()
             gather(0, d, p).start()
-            share(0, q).start()
+            share(0, d * PIECES + p).start()
     for c in load_w(0, 0):
         c.start()
 
     for b in range(BLOCKS):
-        landed(xs.at[b, pl.ds(rows, rows)], dx_r.at[b])
+        landed(xs.at[b, pl.ds(rows, rows)], dx_r.at[b % 2])
 
         def project(i, _, b=b):
             at = b * steps + i
             slot = at % 2
-            for c in load_w(slot, i):
-                c.wait()
+            landed(wgu.at[slot], w_sem.at[slot])
 
             @pl.when(at + 1 < BLOCKS * steps)
             def _():
@@ -160,8 +180,8 @@
 
             run_beside(b, 0, i)
             x = xs[b]
-            gate = jnp.dot(x, wg[slot], preferred_element_type=F32)
-            up = jnp.dot(x, wu[slot], preferred_element_type=F32)
+            gate = jnp.dot(x, wgu[slot, 0], preferred_element_type=F32)
+            up = jnp.dot(x, wgu[slot, 1], preferred_element_type=F32)
             h[:, pl.ds(pl.multiple_of(i * FT, FT), FT)] = (jax.nn.silu(gate) * up).astype(BF16)
             return 0
 
@@ -199,8 +219,9 @@
 
     combine(BLOCKS - 1, NT - 1)
 
-    landed(got.at[0], d0_r)
-    landed(arrived.at[0], n1_r)
+    landed(arrived, ag_s)
+    landed(xs.at[:, pl.ds(0, rows)], dx_s)
+    landed(xs.at[0], own_r)
 
     def early(j, _):
         for d in range(2):
@@ -213,18 +234,18 @@
 
     lax.fori_loop(0, NT, early, 0)
 
-    def finish(j, _):
-        landed(arrived.at[2, :, tile(j)], rs_r.at[1, j])
-        y_ref[:, tile(j)] = (acc[:, tile(j)] + arrived[2, :, tile(j)].astype(F32)).astype(BF16)
-        return 0
-
-    lax.fori_loop(0, NT, finish, 0)
+    def finish(columns):
+        y_ref[:, columns] = (acc[:, columns] + arrived[2, :, columns].astype(F32)).astype(BF16)
+
+    rest = pl.ds(0, depth - LAST)
+    landed(arrived.at[2, :, rest], rs_r.at[1, 0])
+    finish(rest)
+    landed(arrived.at[2, :, last], rs_r.at[1, 1])
+    finish(last)
 
     landed(arrived, rs_s)
-    landed(arrived, ag_s)
     for j in range(2):
         hand(BLOCKS - 1, j).wait_send()
-    landed(xs.at[:, pl.ds(0, rows)], dx_s)
 
 
 def solution(mesh):
@@ -243,8 +264,7 @@
             out_specs=pl.BlockSpec(memory_space=pltpu.VMEM),
             scratch_shapes=[
                 pltpu.VMEM((BLOCKS, 2 * rows, depth), BF16),
-                pltpu.VMEM((2, depth, FT), BF16),
-                pltpu.VMEM((2, depth, FT), BF16),
+                pltpu.VMEM((2, 2, depth, FT), BF16),
                 pltpu.VMEM((2, units, cols), BF16),
                 pltpu.VMEM((2 * rows, units), BF16),
                 pltpu.VMEM((2, rows, cols), F32),
@@ -252,11 +272,11 @@
                 pltpu.VMEM((2, rows, cols), BF16),
                 pltpu.VMEM((BLOCKS, rows, depth), BF16),
                 pltpu.VMEM((3, rows, depth), BF16),
-                dma((2 * PIECES,)), dma((2, 2)), dma((2,)),
+                dma((2,)), dma((2,)), dma((2,)),
                 dma, dma((PIECES + 2,)),
-                dma, dma((BLOCKS,)),
-                dma((2,)), dma, dma((BLOCKS - 1, NT)),
-                dma, dma, dma((2, NT)),
+                dma, dma((2,)),
+                dma((2,)), dma, dma((2, NT)),
+                dma, dma((2, 2)),
             ],
             compiler_params=pltpu.CompilerParams(
                 collective_id=0, has_side_effects=True, vmem_limit_bytes=62914560

time: 142 us -> 142 us (level)
  no operation moved by 1% of the time
where the time goes in v5:
time: 142 us
  Pallas kernels  141 us (99%)
    pallas_call x1, Pallas kernels, step(): pl.pallas_call(functools.partial(kernel, n), name='mlp', out_shape=pltpu....  141 us

profile of v5, /device:TPU:112, one launch (start us, length us, event | category | flops | bytes accessed | tf_op | source)
XLA Modules:
  0.0 142.2 jit_solution(13968745487177066545)
XLA Ops:
  0.0 140.8 %mlp.1 = bf16[256,4096]{1,0:T(8,128)(2,1)S(1)} custom-call(bf16[256,4096]{1,0:T(8,128)(2,1)} %x_ref.1, bf16[4096,1792]{1,0:T(8,128)(2,1)} %wg_ref.1, bf16[4096,1792]{1,0:T(8,128)(2,1)} %wu_ref.1, bf16[1792,4096]{1,0:T(8,128)(2,1)} %wd_ref.1), custom_call_target="tpu_custom_call" | custom-call | tf_op jit(solution)/shard_map/mlp/pallas_call | solution.py:259
  140.8 1.3 copy.6

commit v6 on v5

--- a/solution.py
+++ b/solution.py
@@ -45,7 +45,7 @@
     def gather(s, d, p):
         to = LAND[s][d] * half + p * piece
         if s == 0:
-            src = xs.at[0, pl.ds(d * half + p * piece, piece)]
+            src = x_ref.at[pl.ds(d * half + p * piece, piece)]
         elif s == 1:
             src = xs.at[1, pl.ds(LAND[0][d] * half + p * piece, piece)]
         else:
@@ -148,11 +148,12 @@
             load_x(d * PIECES + p).start()
     pl.semaphore_wait(barrier, 3)
     for p in range(PIECES):
-        if p < 2:
-            landed(xs.at[0, pl.ds(0, 2 * (piece if p == 0 else half - piece))], in_sem.at[p])
         for d in range(2):
             gather(0, d, p).start()
-            share(0, d * PIECES + p).start()
+    for p in range(2):
+        landed(xs.at[0, pl.ds(0, 2 * (piece if p == 0 else half - piece))], in_sem.at[p])
+    for q in range(2 * PIECES):
+        share(0, q).start()
     for c in load_w(0, 0):
         c.start()
 

time: 142 us -> 142 us (level)
  no operation moved by 1% of the time
where the time goes in v6:
time: 142 us
  Pallas kernels  140 us (99%)
    pallas_call x1, Pallas kernels, step(): pl.pallas_call(functools.partial(kernel, n), name='mlp', out_shape=pltpu....  140 us

profile of v6, /device:TPU:112, one launch (start us, length us, event | category | flops | bytes accessed | tf_op | source)
XLA Modules:
  0.0 141.7 jit_solution(15232250980202880834)
XLA Ops:
  0.0 140.4 %mlp.1 = bf16[256,4096]{1,0:T(8,128)(2,1)S(1)} custom-call(bf16[256,4096]{1,0:T(8,128)(2,1)} %x_ref.1, bf16[4096,1792]{1,0:T(8,128)(2,1)} %wg_ref.1, bf16[4096,1792]{1,0:T(8,128)(2,1)} %wu_ref.1, bf16[1792,4096]{1,0:T(8,128)(2,1)} %wd_ref.1), custom_call_target="tpu_custom_call" | custom-call | tf_op jit(solution)/shard_map/mlp/pallas_call | solution.py:260
  140.4 1.3 copy.6

commit v7 on v6

--- a/solution.py
+++ b/solution.py
@@ -10,10 +10,10 @@
 MESH = pl.DeviceIdType.MESH
 BF16, F32 = jnp.bfloat16, jnp.float32
 BLOCKS = 4
-PIECES = 4
+PIECES = 2
 FT = 256
 NT = 4
-LAST = 256
+LAST = 128
 
 LAND = ((1, 0), (0, 1), (1, 0))
 
@@ -128,7 +128,7 @@
         send_on(b - 1, j)
 
     beside = {
-        (0, 0, 2): [(0, 0)], (0, 0, 5): [(0, 1)], (0, 1, 0): [(0, 2)], (0, 1, 2): [(0, 3)],
+        (0, 0, 6): [(0, 0)], (0, 1, 2): [(0, 1)],
         (1, 1, 1): [(1, 0)], (2, 0, 6): [(2, 0)],
     }
 

time: 142 us -> 142 us (level)
  no operation moved by 1% of the time
where the time goes in v7:
time: 142 us
  Pallas kernels  140 us (99%)
    pallas_call x1, Pallas kernels, step(): pl.pallas_call(functools.partial(kernel, n), name='mlp', out_shape=pltpu....  140 us

profile of v7, /device:TPU:112, one launch (start us, length us, event | category | flops | bytes accessed | tf_op | source)
XLA Modules:
  0.0 141.7 jit_solution(368882246511455732)
XLA Ops:
  0.0 140.4 %mlp.1 = bf16[256,4096]{1,0:T(8,128)(2,1)S(1)} custom-call(bf16[256,4096]{1,0:T(8,128)(2,1)} %x_ref.1, bf16[4096,1792]{1,0:T(8,128)(2,1)} %wg_ref.1, bf16[4096,1792]{1,0:T(8,128)(2,1)} %wu_ref.1, bf16[1792,4096]{1,0:T(8,128)(2,1)} %wd_ref.1), custom_call_target="tpu_custom_call" | custom-call | tf_op jit(solution)/shard_map/mlp/pallas_call | solution.py:260
  140.4 1.3 copy.6
